TPU v7x, 32 devices: a whole 2x2x4 slice. The times are simulated.
32 devices in a mesh: grp: 4 (over y, x), sub: 8 (over z, core).
Axes of the slice: x: 2, y: 2, z: 4, core: 2. Of those that a mesh axis runs over, the one named last changes fastest.
Arguments:
- bem_tiles: float32 [4096, 4096], P('grp', 'sub'), may hold values from -0.0625 to 0.0625
- leaf_inverse: float32 [4, 16, 1024, 1024], P('grp', 'sub'), may hold values from -1.5 to 1.5
- coupling: float32 [4, 16, 1024, 512], P('grp', 'sub'), may hold values from -0.0625 to 0.0625
- schur_inverse: float32 [4, 512, 512], P('grp', None, 'sub'), may hold values from -1.5 to 1.5
- leaf_load: float32 [4, 16, 1024, 128], P('grp', 'sub'), may hold values from -6 to 6
- sep_load: float32 [4, 512, 128], P('grp'), may hold values from -6 to 6
- surf_load: float32 [4096, 128], P(('grp', 'sub')), may hold values from -6 to 6
- surf_start: float32 [4096, 128], P(('grp', 'sub')), may hold values from -6 to 6
- flux_weight: float32 [4, 16, 8, 128], P('grp', 'sub'), may hold values from 0.25 to 1
- trace_weight: float32 [4, 16, 8, 128], P('grp', 'sub'), may hold values from 0.25 to 1
- leaf_sizes: int32 [4, 16], P('grp', 'sub'), may hold values from 512 to 1024
- block_counts: int32 [4, 16], P('grp', 'sub'), may hold values from 4 to 8
- block_owner: int32 [4, 16, 8, 1], P('grp', 'sub'), may hold values from 0 to 7; in each aligned block of 16 rows (0 to 15, 16 to 31, ..., all dimensions but the last counted through in order) at most 2 rows name the same one
Outputs:
- solution: float32 [4, 16, 1024, 128], P('grp', 'sub')
- sep_value: float32 [4, 512, 128], P('grp', 'sub')
- pressure: float32 [4096, 128], P(('grp', 'sub'))
Inputs may be any that keep to these rules, and one draw needn't show every extreme that they name: `block_owner`: of the 16 entries of one device, live or not, at most 2 name the same owner, and some device has 2 entries naming one owner.
All inputs are finite; a program needn't handle non-finite values.
Results may differ from a plain program's by a relative error of at most 0.00018.
Values sent between devices are 32-bit elements; how exact they have to be, the bound alone decides.
A program may use at most 128 MiB of HBM per device.

v0:
```python
import jax
import jax.numpy as jnp
from jax import lax
from jax.sharding import PartitionSpec as P

CAP = 2
SWEEPS = 3


def on_device(
    bem_tiles,
    leaf_inverse,
    coupling,
    schur_inverse,
    leaf_load,
    sep_load,
    surf_load,
    surf_start,
    flux_weight,
    trace_weight,
    leaf_sizes,
    block_counts,
    block_owner,
):
    highest = lax.Precision.HIGHEST
    parts = lax.axis_size("sub")
    here = lax.axis_index("sub")
    width = surf_load.shape[0]
    loads = surf_load.shape[1]
    leaves = leaf_inverse.shape[1]
    order = leaf_inverse.shape[2]
    blocks = order // width
    entries = leaves * blocks
    separator = schur_inverse.shape[1]
    sep_share = schur_inverse.shape[2]
    row_mask = (jnp.arange(order, dtype=jnp.int32)[None, :] < leaf_sizes[0][:, None]).astype(
        jnp.float32
    )[:, :, None]
    active = (
        (jnp.arange(blocks, dtype=jnp.int32)[None, :] < block_counts[0][:, None])
        .astype(jnp.float32)
        .reshape(entries)
    )
    owner = block_owner[0, :, :, 0].reshape(entries)
    picker = (owner[:, None] == jnp.arange(parts, dtype=jnp.int32)[None, :]).astype(jnp.float32)
    live_pick = picker * active[:, None]
    flux_scale = flux_weight[0].reshape(entries, width)[:, :, None]
    trace_scale = (trace_weight[0].reshape(entries, width) * active[:, None])[:, :, None]
    position = jnp.arange(entries, dtype=jnp.int32)
    earlier = (position[:, None] > position[None, :]) & (owner[:, None] == owner[None, :])
    slot_index = jnp.sum(earlier.astype(jnp.int32), axis=1)
    target = owner * CAP + slot_index
    placing = (jnp.arange(parts * CAP, dtype=jnp.int32)[:, None] == target[None, :]).astype(
        jnp.float32
    )
    schur_full = lax.all_gather(schur_inverse[0], "sub", axis=1, tiled=True)
    pressure = surf_start
    sep_value = jnp.zeros((separator, loads), jnp.float32)
    solution = jnp.zeros((leaves, order, loads), jnp.float32)
    for sweep in range(SWEEPS):
        column = lax.all_gather(pressure, "grp", axis=0, tiled=True)

        def tile_product(start, count, column=column):
            return jnp.dot(bem_tiles, column, precision=highest, preferred_element_type=jnp.float32)

        applied = lax.psum_scatter(
            tile_product(jnp.int32(0), lax.axis_size("sub") * width),
            "sub",
            scatter_dimension=0,
            tiled=True,
        )
        surface_patch = lax.all_gather(pressure, "sub", axis=0, tiled=True).reshape(
            parts, width, loads
        )
        flux = jnp.einsum("eo,oil->eil", live_pick, surface_patch, precision=highest) * flux_scale
        flux = flux.reshape(leaves, order, loads)
        pulled = jnp.einsum("jrs,sl->jrl", coupling[0], sep_value, precision=highest)
        rhs = (leaf_load[0] - pulled - flux) * row_mask
        solution = jnp.einsum("jrc,jcl->jrl", leaf_inverse[0], rhs, precision=highest) * row_mask
        partial_sum = jnp.einsum("jrs,jrl->sl", coupling[0], solution, precision=highest)
        summed = lax.psum(partial_sum, "sub")
        sep_value = jnp.dot(
            schur_full, sep_load[0] - summed, precision=highest, preferred_element_type=jnp.float32
        )
        weighted = solution.reshape(entries, width, loads) * trace_scale
        outgoing = jnp.dot(
            placing,
            weighted.reshape(entries, width * loads),
            precision=highest,
            preferred_element_type=jnp.float32,
        )
        incoming = lax.all_to_all(
            outgoing.reshape(parts, CAP, width, loads),
            "sub",
            split_axis=0,
            concat_axis=0,
            tiled=True,
        )
        trace = jnp.sum(incoming, axis=(0, 1))
        pressure = surf_load + applied + trace
    sep_rows_out = lax.dynamic_slice_in_dim(sep_value, here * sep_share, sep_share, 0)
    return (solution[None], sep_rows_out[None], pressure)


def solution(mesh):
    return jax.shard_map(
        on_device,
        mesh=mesh,
        in_specs=(
            P("grp", "sub"),
            P("grp", "sub", None, None),
            P("grp", "sub", None, None),
            P("grp", None, "sub"),
            P("grp", "sub", None, None),
            P("grp", None, None),
            P(("grp", "sub"), None),
            P(("grp", "sub"), None),
            P("grp", "sub", None, None),
            P("grp", "sub", None, None),
            P("grp", "sub"),
            P("grp", "sub"),
            P("grp", "sub", None, None),
        ),
        out_specs=(P("grp", "sub", None, None), P("grp", "sub", None), P(("grp", "sub"), None)),
        check_vma=False,
    )
```

profile of v0, /device:TPU:0, one launch (start us, length us, event | category | flops | bytes accessed | tf_op | source)
XLA Modules:
  0.0 464.7 jit_solution(11380869395240890339)
XLA Ops:
  7.3 10.9 %all_gather.23 = f32[512,128]{1,0:T(8,128)S(1)} all-gather(f32[128,128]{1,0:T(8,128)} %param.20), channel_id=1, replica_groups=mesh['grp'=4,'sub'=8] {'grp'}, dimensions={0}, use_global_device_ids=true | all-gather | bytes 327680 | tf_op jit(solution)/shard_map/all_gather | solution.py:61
  18.2 2.6 fusion.127
  20.8 15.6 %all_gather.21 = f32[1024,128]{1,0:T(8,128)S(1)} all-gather(f32[128,128]{1,0:T(8,128)} %param.20), channel_id=1, replica_groups=mesh['grp'=4,'sub'=8] {'sub'}, dimensions={0}, use_global_device_ids=true | all-gather | bytes 589824 | tf_op jit(solution)/shard_map/all_gather | solution.py:72
  38.2 1.2 convolution_multiply_fusion.2
  39.7 1.3 copy.80
  41.0 1.6 copy.75
  42.6 7.2 %fusion.51 = f32[2,1024,128]{1,2,0:T(8,128)S(1)} fusion(f32[2,1024,128]{1,2,0:T(8,128)} %copy.80, f32[1,2,1024,512]{3,2,1,0:T(8,128)} %param.15, f32[1,2,1024,128]{2,3,1,0:T(8,128)S(1)} %copy.75, f32[2,1024]{1,0:T(2,128)S(1)} %compare_convert_fusion), kind=kOutput, calls=%fused_computation.29 | convolution fusion | flops 1611399168 | bytes 7348224 | tf_op jit(solution)/shard_map/jrs,sl->jrl/dot_general | solution.py:77
  49.8 12.1 %fusion.57 = f32[2,1024,128]{1,2,0:T(8,128)} fusion(f32[2,1024,128]{1,2,0:T(8,128)S(1)} %fusion.51, f32[1,2,1024,1024]{3,2,1,0:T(8,128)} %param.14, f32[2,1024]{1,0:T(2,128)S(1)} %compare_convert_fusion), kind=kOutput, calls=%fused_computation.34 | convolution fusion | flops 3221487616 | bytes 10493952 | tf_op jit(solution)/shard_map/jrc,jcl->jrl/dot_general | solution.py:79
  62.0 1.6 copy.81
  63.5 1.2 reshape.163
  65.0 2.4 fusion.85
  67.5 1.2 copy.83
  68.7 5.2 %all-to-all-start = ((f32[8,2,128,128]{3,2,1,0:T(8,128)}), f32[8,2,128,128]{3,2,1,0:T(8,128)}, u32[]{:S(2)}, u32[]{:S(2)}) async-start(f32[8,2,128,128]{3,2,1,0:T(8,128)} %copy.83), calls=%async_computation.1 | async-start | bytes 2097152 | tf_op jit(solution)/shard_map/all_to_all | solution.py:92
  74.3 5.7 %fusion.69 = f32[512,128]{0,1:T(8,128)} fusion(f32[2,1024,128]{1,2,0:T(8,128)} %fusion.57, f32[1,2,1024,512]{3,2,1,0:T(8,128)} %param.15), kind=kOutput, calls=%fused_computation.40 | convolution fusion | flops 1610612736 | bytes 5505024 | tf_op jit(solution)/shard_map/jrs,jrl->sl/dot_general | solution.py:80
  80.7 1.1 copy.76
  81.8 20.1 %all-to-all-done = f32[8,2,128,128]{3,2,1,0:T(8,128)} async-done(((f32[8,2,128,128]{3,2,1,0:T(8,128)}), f32[8,2,128,128]{3,2,1,0:T(8,128)}, u32[]{:S(2)}, u32[]{:S(2)}) %all-to-all-start) | async-done | bytes 1048608 | tf_op jit(solution)/shard_map/all_to_all | solution.py:92
  101.9 1.9 reduce_sum.37
  103.9 0.9 add_add_fusion.2
  104.8 14.8 %all_gather.24 = f32[1024,128]{1,0:T(8,128)S(1)} all-gather(f32[128,128]{1,0:T(8,128)S(1)} %add_add_fusion.2), channel_id=1, replica_groups=mesh['grp'=4,'sub'=8] {'sub'}, dimensions={0}, use_global_device_ids=true | all-gather | bytes 589824 | tf_op jit(solution)/shard_map/all_gather | solution.py:72
  119.5 1.8 convolution_multiply_fusion.1
  121.4 1.3 copy.85
  122.7 2.6 copy.86
  125.2 15.9 %all-reduce.4.cloned.1.call-done = f32[512,128]{0,1:T(8,128)} async-done(((f32[512,128]{0,1:T(8,128)}), f32[512,128]{0,1:T(8,128)}) %all-reduce.4.cloned.1.call-update) | async-done | bytes 262160 | tf_op jit(solution)/shard_map/psum | solution.py:81
  141.2 22.9 %all-gather.3.cloned.1.call-done = f32[1,512,512]{1,2,0:T(8,128)} async-done(((f32[1,512,64]{1,2,0:T(8,128)}), f32[1,512,512]{1,2,0:T(8,128)}) %all-gather.3.cloned.1.call-update) | async-done | bytes 1048592 | tf_op jit(solution)/shard_map/all_gather | solution.py:56
  164.1 2.0 convolution_bitcast_fusion.3
  166.1 7.2 %fusion.42 = f32[2,1024,128]{1,2,0:T(8,128)S(1)} fusion(f32[2,1024,128]{1,2,0:T(8,128)} %copy.86, f32[128,512,1]{1,0,2:T(8,128)S(1)} %convolution_bitcast_fusion.3, f32[1,2,1024,512]{3,2,1,0:T(8,128)} %param.15, f32[1,2,1024,128]{2,3,1,0:T(8,128)} %copy-done.2, f32[2,1024]{1,0:T(2,128)S(1)} %compare_convert_fusion), kind=kOutput, calls=%fused_computation.26 | convolution fusion | flops 1611399168 | bytes 7610368 | tf_op jit(solution)/shard_map/jrs,sl->jrl/dot_general | solution.py:77
  173.3 12.1 %fusion.63 = f32[2,1024,128]{1,2,0:T(8,128)} fusion(f32[2,1024,128]{1,2,0:T(8,128)S(1)} %fusion.42, f32[1,2,1024,1024]{3,2,1,0:T(8,128)} %param.14, f32[2,1024]{1,0:T(2,128)S(1)} %compare_convert_fusion), kind=kOutput, calls=%fused_computation.36 | convolution fusion | flops 3221487616 | bytes 10493952 | tf_op jit(solution)/shard_map/jrc,jcl->jrl/dot_general | solution.py:79
  185.4 2.6 copy.88
  188.0 2.4 reshape.166
  190.4 2.5 fusion.83
  192.8 1.2 copy.90
  194.0 4.2 all-to-all-start.1
  198.5 5.7 %fusion.72 = f32[512,128]{0,1:T(8,128)} fusion(f32[2,1024,128]{1,2,0:T(8,128)} %fusion.63, f32[1,2,1024,512]{3,2,1,0:T(8,128)} %param.15), kind=kOutput, calls=%fused_computation.41 | convolution fusion | flops 1610612736 | bytes 5505024 | tf_op jit(solution)/shard_map/jrs,jrl->sl/dot_general | solution.py:80
  204.2 9.0 %all_gather.25 = f32[512,128]{1,0:T(8,128)S(1)} all-gather(f32[128,128]{1,0:T(8,128)S(1)} %add_add_fusion.2), channel_id=1, replica_groups=mesh['grp'=4,'sub'=8] {'grp'}, dimensions={0}, use_global_device_ids=true | all-gather | bytes 327680 | tf_op jit(solution)/shard_map/all_gather | solution.py:61
  213.2 3.1 convolution_bitcast_fusion.1
  216.3 1.6 copy.87
  217.9 48.1 %all-reduce.6.cloned.1.call-done = f32[512,128]{0,1:T(8,128)} async-done(((f32[512,128]{0,1:T(8,128)}), f32[512,128]{0,1:T(8,128)}) %all-reduce.6.cloned.1.call-update) | async-done | bytes 262160 | tf_op jit(solution)/shard_map/psum | solution.py:81
  266.0 2.7 convolution_bitcast_fusion.2
  268.8 1.3 reduce_sum.38
  270.1 0.7 copy.92
  270.8 28.2 %reduce-scatter.6.cloned.1.call-done = f32[128,128]{0,1:T(8,128)} async-done(((f32[1024,128]{0,1:T(8,128)}), f32[128,128]{0,1:T(8,128)}) %reduce-scatter.6.cloned.1.call-update) | async-done | bytes 65552 | tf_op jit(solution)/shard_map/reduce_scatter | solution.py:66
  299.0 0.9 add_add_fusion.1
  299.9 14.9 %all_gather.26 = f32[1024,128]{0,1:T(8,128)S(1)} all-gather(f32[128,128]{0,1:T(8,128)S(1)} %add_add_fusion.1), channel_id=1, replica_groups=mesh['grp'=4,'sub'=8] {'sub'}, dimensions={0}, use_global_device_ids=true | all-gather | bytes 589824 | tf_op jit(solution)/shard_map/all_gather | solution.py:72
  314.8 0.9 copy.111
  315.7 2.0 copy.93
  317.8 2.1 convolution_multiply_fusion
  319.8 1.3 copy.94
  321.1 2.6 copy.95
  323.7 7.2 %fusion.33 = f32[2,1024,128]{1,2,0:T(8,128)S(1)} fusion(f32[2,1024,128]{1,2,0:T(8,128)} %copy.95, f32[128,512,1]{1,0,2:T(8,128)} %convolution_bitcast_fusion.2, f32[1,2,1024,512]{3,2,1,0:T(8,128)} %param.15, f32[1,2,1024,128]{2,3,1,0:T(8,128)} %copy-done.2, f32[2,1024]{1,0:T(2,128)S(1)} %compare_convert_fusion), kind=kOutput, calls=%fused_computation.23 | convolution fusion | flops 1611399168 | bytes 7610368 | tf_op jit(solution)/shard_map/jrs,sl->jrl/dot_general | solution.py:77
  330.9 12.1 %fusion.66 = f32[2,128,1024]{2,1,0:T(8,128)} fusion(f32[2,1024,128]{1,2,0:T(8,128)S(1)} %fusion.33, f32[1,2,1024,1024]{3,2,1,0:T(8,128)} %param.14, f32[2,1024]{1,0:T(2,128)S(1)} %compare_convert_fusion), kind=kOutput, calls=%fused_computation.37 | convolution fusion | flops 3221487616 | bytes 10493952 | tf_op jit(solution)/shard_map/jrc,jcl->jrl/dot_general | solution.py:79
  343.0 2.6 copy.97
  345.7 2.4 reshape.169
  348.1 2.4 fusion.81
  350.5 1.2 copy.99
  351.7 4.2 all-to-all-start.2
  356.2 5.3 %fusion.75 = f32[512,128]{0,1:T(8,128)} fusion(f32[1,2,1024,512]{3,2,1,0:T(8,128)} %param.15, f32[2,128,1024]{2,1,0:T(8,128)S(1)} %copy-done.1), kind=kOutput, calls=%fused_computation.42 | convolution fusion | flops 1610612736 | bytes 5505024 | tf_op jit(solution)/shard_map/jrs,jrl->sl/dot_general | solution.py:80
  361.6 10.3 %all_gather.27 = f32[512,128]{0,1:T(8,128)S(1)} all-gather(f32[128,128]{0,1:T(8,128)S(1)} %add_add_fusion.1), channel_id=1, replica_groups=mesh['grp'=4,'sub'=8] {'grp'}, dimensions={0}, use_global_device_ids=true | all-gather | bytes 327680 | tf_op jit(solution)/shard_map/all_gather | solution.py:61
  371.9 3.1 convolution_bitcast_fusion
  375.0 1.3 copy.102
  376.3 47.2 %all-reduce.8.cloned.1.call-done = f32[512,128]{0,1:T(8,128)} async-done(((f32[512,128]{0,1:T(8,128)}), f32[512,128]{0,1:T(8,128)}) %all-reduce.8.cloned.1.call-update) | async-done | bytes 262160 | tf_op jit(solution)/shard_map/psum | solution.py:81
  423.6 3.1 fusion.87
  427.3 1.3 reduce_sum.39
  428.7 27.4 %reduce-scatter.8.cloned.1.call-done = f32[128,128]{0,1:T(8,128)} async-done(((f32[1024,128]{0,1:T(8,128)}), f32[128,128]{0,1:T(8,128)}) %reduce-scatter.8.cloned.1.call-update) | async-done | bytes 65552 | tf_op jit(solution)/shard_map/reduce_scatter | solution.py:66
  456.1 0.9 add_add_fusion
  (57 shorter events, 5.9 us)
Async XLA Ops:
  7.2 11.0 %copy-start = (f32[1024,512]{1,0:T(8,128)S(1)}, f32[1024,512]{1,0:T(8,128)}, u32[]{:S(2)}) copy-start(f32[1024,512]{1,0:T(8,128)} %param.13) | copy-start | bytes 6291460
  7.2 29.7 %copy-start.9 = (s32[1,2,8,1]{2,3,1,0:T(1,128)S(1)}, s32[1,2,8,1]{2,3,1,0:T(1,128)}, u32[]{:S(2)}) copy-start(s32[1,2,8,1]{2,3,1,0:T(1,128)} %param.25) | copy-start | bytes 196
  7.2 30.6 %copy-start.11 = (s32[1,2]{1,0:T(1,128)S(1)}, s32[1,2]{1,0:T(1,128)}, u32[]{:S(2)}) copy-start(s32[1,2]{1,0:T(1,128)} %param.24) | copy-start | bytes 28
  7.2 30.8 %copy-start.10 = (s32[1,2]{1,0:T(1,128)S(1)}, s32[1,2]{1,0:T(1,128)}, u32[]{:S(2)}) copy-start(s32[1,2]{1,0:T(1,128)} %param.23) | copy-start | bytes 28
  7.2 30.8 %copy-start.4 = (f32[1,2,8,128]{3,2,1,0:T(8,128)S(1)}, f32[1,2,8,128]{3,2,1,0:T(8,128)}, u32[]{:S(2)}) copy-start(f32[1,2,8,128]{3,2,1,0:T(8,128)} %param.21) | copy-start | bytes 24580
  7.2 30.9 %copy-start.5 = (f32[1,2,8,128]{3,2,1,0:T(8,128)S(1)}, f32[1,2,8,128]{3,2,1,0:T(8,128)}, u32[]{:S(2)}) copy-start(f32[1,2,8,128]{3,2,1,0:T(8,128)} %param.22) | copy-start | bytes 24580
  7.2 96.6 %reduce-scatter.4.cloned.1.call-start = ((), (), s32[]{:S(2)}) async-start(), calls=%async_computation.7 | async-start | bytes 589824 | tf_op jit(solution)/shard_map/reduce_scatter | solution.py:66
  37.6 24.3 %copy-start.6 = (s32[16]{0:T(128)}, s32[16]{0:T(128)S(1)}, u32[]{:S(2)}) copy-start(s32[16]{0:T(128)S(1)} %eq.58) | copy-start | bytes 196
  42.6 19.3 %copy-start.2 = (f32[1,2,1024,128]{2,3,1,0:T(8,128)}, f32[1,2,1024,128]{2,3,1,0:T(8,128)S(1)}, u32[]{:S(2)}) copy-start(f32[1,2,1024,128]{2,3,1,0:T(8,128)S(1)} %copy.75) | copy-start | bytes 3145732
  61.9 5.5 %copy-start.7 = (s32[16]{0:T(128)}, s32[16]{0:T(128)S(1)}, u32[]{:S(2)}) copy-start(s32[16]{0:T(128)S(1)} %multiply_add_fusion.1) | copy-start | bytes 196
  68.7 33.3 %all-to-all-start = ((f32[8,2,128,128]{3,2,1,0:T(8,128)}), f32[8,2,128,128]{3,2,1,0:T(8,128)}, u32[]{:S(2)}, u32[]{:S(2)}) async-start(f32[8,2,128,128]{3,2,1,0:T(8,128)} %copy.83), calls=%async_computation.1 | async-start | bytes 2097152 | tf_op jit(solution)/shard_map/all_to_all | solution.py:92
  73.8 67.3 %all-reduce.4.cloned.1.call-start = ((), (), s32[]{:S(2)}) async-start(), calls=%async_computation.6 | async-start | bytes 524288 | tf_op jit(solution)/shard_map/psum | solution.py:81
  80.0 84.1 %all-gather.3.cloned.1.call-start = ((), (), s32[]{:S(2)}) async-start(), calls=%async_computation.12 | async-start | bytes 1179648 | tf_op jit(solution)/shard_map/all_gather | solution.py:56
  194.0 74.8 %all-to-all-start.1 = ((f32[8,2,128,128]{3,2,1,0:T(8,128)}), f32[8,2,128,128]{3,2,1,0:T(8,128)}, u32[]{:S(2)}, u32[]{:S(2)}) async-start(f32[8,2,128,128]{3,2,1,0:T(8,128)} %copy.90), calls=%async_computation.3 | async-start | bytes 2097152 | tf_op jit(solution)/shard_map/all_to_all | solution.py:92
  198.3 67.8 %all-reduce.6.cloned.1.call-start = ((), (), s32[]{:S(2)}) async-start(), calls=%async_computation.8 | async-start | bytes 524288 | tf_op jit(solution)/shard_map/psum | solution.py:81
  204.2 94.8 %reduce-scatter.6.cloned.1.call-start = ((), (), s32[]{:S(2)}) async-start(), calls=%async_computation.9 | async-start | bytes 589824 | tf_op jit(solution)/shard_map/reduce_scatter | solution.py:66
  343.0 5.0 %copy-start.8 = (s32[16]{0:T(128)S(1)}, s32[16]{0:T(128)}, u32[]{:S(2)}) copy-start(s32[16]{0:T(128)} %copy-done.7) | copy-start | bytes 196
  350.5 5.7 %copy-start.1 = (f32[2,128,1024]{2,1,0:T(8,128)S(1)}, f32[2,128,1024]{2,1,0:T(8,128)}, u32[]{:S(2)}) copy-start(f32[2,128,1024]{2,1,0:T(8,128)} %fusion.66) | copy-start | bytes 3145732
  351.7 75.6 %all-to-all-start.2 = ((f32[8,2,128,128]{3,2,1,0:T(8,128)}), f32[8,2,128,128]{3,2,1,0:T(8,128)}, u32[]{:S(2)}, u32[]{:S(2)}) async-start(f32[8,2,128,128]{3,2,1,0:T(8,128)} %copy.99), calls=%async_computation.5 | async-start | bytes 2097152 | tf_op jit(solution)/shard_map/all_to_all | solution.py:92
  356.0 67.6 %all-reduce.8.cloned.1.call-start = ((), (), s32[]{:S(2)}) async-start(), calls=%async_computation.10 | async-start | bytes 524288 | tf_op jit(solution)/shard_map/psum | solution.py:81
  361.6 94.5 %reduce-scatter.8.cloned.1.call-start = ((), (), s32[]{:S(2)}) async-start(), calls=%async_computation.11 | async-start | bytes 589824 | tf_op jit(solution)/shard_map/reduce_scatter | solution.py:66
  371.9 84.2 %copy-start.3 = (f32[128,128]{0,1:T(8,128)S(1)}, f32[128,128]{0,1:T(8,128)}, u32[]{:S(2)}) copy-start(f32[128,128]{0,1:T(8,128)} %copy.87) | copy-start | bytes 196612
Sparse Core Ops, SparseCore 0:
  20.9 31.6 reduce-scatter.3
  80.1 61.0 all-reduce.3
  142.8 21.2 all-gather.2
  204.3 61.7 all-reduce.5
  268.7 30.1 reduce-scatter.5
  361.7 61.8 all-reduce.7
  425.8 30.1 reduce-scatter.7
where the time goes:
time: 468 us; the launch traced here: 465 us
  waiting for transfers between devices  211 us (45%)
  matrix products  104 us (22%)
  blocking collectives  75.4 us (16%)
  local copies, waits for them, and re-layouts  37.4 us (8%)
  starting transfers between devices  14.7 us (3%)
  between operations  14.6 us (3%)
  other arithmetic  8.24 us (2%)
    psum x3, waiting for transfers between devices, on_device(): summed = lax.psum(partial_sum, 'sub')  111 us
    reduce_scatter x3, waiting for transfers between devices, on_device(): lax.psum_scatter(tile_product(jnp.int32(0), lax.axis_size('sub') * width)...  55.5 us
    all_gather x3, blocking collectives, on_device(): lax.all_gather(pressure, 'sub', axis=0, tiled=True)  45.3 us
    dot_general x3, matrix products, on_device(): jnp.einsum('jrc,jcl->jrl', leaf_inverse[0], rhs, precision=highest)  36.3 us
    all_gather x3, blocking collectives, on_device(): column = lax.all_gather(pressure, 'grp', axis=0, tiled=True)  30.1 us
    all_gather x1, waiting for transfers between devices, on_device(): schur_full = lax.all_gather(schur_inverse[0], 'sub', axis=1, tiled=True)  22.9 us
    dot_general x3, matrix products, on_device(): jnp.einsum('jrs,sl->jrl', coupling[0], sep_value, precision=highest)  21.6 us
    all_to_all x3, waiting for transfers between devices, on_device(): lax.all_to_all(outgoing.reshape(parts, CAP, width, loads), 'sub', split_a...  20.1 us
  transfers between devices with their start and end apart: 10, of which 7 were waited for; matrix products, arithmetic and copies ran while one was open for 17% of the time, Pallas kernels for 0%

commit v1 on v0

--- a/solution.py
+++ b/solution.py
@@ -78,7 +78,7 @@
         rhs = (leaf_load[0] - pulled - flux) * row_mask
         solution = jnp.einsum("jrc,jcl->jrl", leaf_inverse[0], rhs, precision=highest) * row_mask
         partial_sum = jnp.einsum("jrs,jrl->sl", coupling[0], solution, precision=highest)
-        summed = lax.psum(partial_sum, "sub")
+        summed = jnp.sum(lax.all_gather(partial_sum, "sub"), axis=0)
         sep_value = jnp.dot(
             schur_full, sep_load[0] - summed, precision=highest, preferred_element_type=jnp.float32
         )

time: 468 us -> 382 us (0.82)
  waiting for transfers between devices: 211 us -> 115 us
  local copies, waits for them, and re-layouts: 37.4 us -> 52 us
  matrix products: 104 us -> 89.5 us
    psum x3 -> x0, waiting for transfers between devices: 111 us -> none  [on_device(): summed = lax.psum(partial_sum, 'sub')]
    all_to_all x3, waiting for transfers between devices: 20.1 us -> 114 us  [on_device(): lax.all_to_all(outgoing.reshape(parts, CAP, width, loads), 'sub', split_a...]
    reduce_scatter x3, waiting for transfers between devices: 55.5 us -> 0.01 us  [on_device(): lax.psum_scatter(tile_product(jnp.int32(0), lax.axis_size('sub') * width)...]
    all_gather x1, waiting for transfers between devices: 22.9 us -> 0.01 us  [on_device(): schur_full = lax.all_gather(schur_inverse[0], 'sub', axis=1, tiled=True)]
    unnamed x31 -> x56, local copies, waits for them, and re-layouts: 7.7 us -> 19.7 us
    dot_general x3, matrix products: 16.6 us -> 9.48 us  [on_device(): jnp.einsum('jrs,jrl->sl', coupling[0], solution, precision=highest)]
  transfers between devices with their start and end apart: 10 -> 10, of which waited for: 7 -> 3; matrix products, arithmetic and copies ran while one was open for 17% -> 37% of each run, Pallas kernels for 0% -> 0%
where the time goes in v1:
time: 382 us; the launch traced here: 375 us
  waiting for transfers between devices  115 us (30%)
  matrix products  89.5 us (23%)
  blocking collectives  78.4 us (21%)
  local copies, waits for them, and re-layouts  52 us (14%)
  between operations  15.1 us (4%)
  starting transfers between devices  14.3 us (4%)
  other arithmetic  10.6 us (3%)
    all_to_all x3, waiting for transfers between devices, on_device(): lax.all_to_all(outgoing.reshape(parts, CAP, width, loads), 'sub', split_a...  114 us
    all_gather x3, blocking collectives, on_device(): lax.all_gather(pressure, 'sub', axis=0, tiled=True)  47.7 us
    dot_general x3, matrix products, on_device(): jnp.einsum('jrc,jcl->jrl', leaf_inverse[0], rhs, precision=highest)  34.2 us
    all_gather x3, blocking collectives, on_device(): column = lax.all_gather(pressure, 'grp', axis=0, tiled=True)  30.8 us
    unnamed x56, local copies, waits for them, and re-layouts  19.7 us
    dot_general x3, matrix products, on_device(): jnp.einsum('jrs,sl->jrl', coupling[0], sep_value, precision=highest)  18.9 us
    all_to_all x3, starting transfers between devices, on_device(): lax.all_to_all(outgoing.reshape(parts, CAP, width, loads), 'sub', split_a...  14.1 us
    dot_general x3, matrix products, on_device(): jnp.einsum('jrs,jrl->sl', coupling[0], solution, precision=highest)  9.48 us
  transfers between devices with their start and end apart: 10, of which 3 were waited for; matrix products, arithmetic and copies ran while one was open for 37% of the time, Pallas kernels for 0%

profile of v1, /device:TPU:0, one launch (start us, length us, event | category | flops | bytes accessed | tf_op | source)
XLA Modules:
  0.0 375.0 jit_solution(15609165641557830710)
XLA Ops:
  7.3 10.9 %all_gather.43 = f32[512,128]{1,0:T(8,128)S(1)} all-gather(f32[128,128]{1,0:T(8,128)} %param.20), channel_id=1, replica_groups=mesh['grp'=4,'sub'=8] {'grp'}, dimensions={0}, use_global_device_ids=true | all-gather | bytes 327680 | tf_op jit(solution)/shard_map/all_gather | solution.py:61
  18.1 2.6 fusion.127
  20.8 16.3 %all_gather.39 = f32[1024,128]{1,0:T(8,128)} all-gather(f32[128,128]{1,0:T(8,128)} %param.20), channel_id=1, replica_groups=mesh['grp'=4,'sub'=8] {'sub'}, dimensions={0}, use_global_device_ids=true | all-gather | bytes 589824 | tf_op jit(solution)/shard_map/all_gather | solution.py:72
  38.6 2.2 convolution_multiply_fusion.2
  40.9 1.3 copy.79
  42.1 2.5 copy.80
  44.8 1.6 copy.75
  46.3 7.2 %fusion.51 = f32[2,1024,128]{1,2,0:T(8,128)S(1)} fusion(f32[2,1024,128]{1,2,0:T(8,128)} %copy.80, f32[1,2,1024,512]{3,2,1,0:T(8,128)} %param.15, f32[1,2,1024,128]{2,3,1,0:T(8,128)S(1)} %copy.75, f32[2,1024]{1,0:T(2,128)S(1)} %compare_convert_fusion), kind=kOutput, calls=%fused_computation.32 | convolution fusion | flops 1611399168 | bytes 7348224 | tf_op jit(solution)/shard_map/jrs,sl->jrl/dot_general | solution.py:77
  53.6 11.4 %fusion.57 = f32[2,1024,128]{1,2,0:T(8,128)S(1)} fusion(f32[2,1024,128]{1,2,0:T(8,128)S(1)} %fusion.51, f32[1,2,1024,1024]{3,2,1,0:T(8,128)} %param.14, f32[2,1024]{1,0:T(2,128)S(1)} %compare_convert_fusion), kind=kOutput, calls=%fused_computation.37 | convolution fusion | flops 3221487616 | bytes 10493952 | tf_op jit(solution)/shard_map/jrc,jcl->jrl/dot_general | solution.py:79
  65.1 1.0 copy-done.10
  66.0 3.2 fusion.69
  69.2 1.6 copy.81
  70.8 1.2 reshape.163
  72.6 2.4 fusion.85
  75.0 1.2 copy.83
  76.2 5.3 %all-to-all-start = ((f32[8,2,128,128]{3,2,1,0:T(8,128)}), f32[8,2,128,128]{3,2,1,0:T(8,128)}, u32[]{:S(2)}, u32[]{:S(2)}) async-start(f32[8,2,128,128]{3,2,1,0:T(8,128)} %copy.83), calls=%async_computation.1 | async-start | bytes 2097152 | tf_op jit(solution)/shard_map/all_to_all | solution.py:92
  82.2 1.1 copy.76
  83.3 37.0 %all-to-all-done = f32[8,2,128,128]{3,2,1,0:T(8,128)} async-done(((f32[8,2,128,128]{3,2,1,0:T(8,128)}), f32[8,2,128,128]{3,2,1,0:T(8,128)}, u32[]{:S(2)}, u32[]{:S(2)}) %all-to-all-start) | async-done | bytes 1048608 | tf_op jit(solution)/shard_map/all_to_all | solution.py:92
  120.3 1.9 reduce_sum.65
  122.2 0.9 add_add_fusion.2
  123.2 16.6 %all_gather.44 = f32[1024,128]{1,0:T(8,128)S(1)} all-gather(f32[128,128]{1,0:T(8,128)S(1)} %add_add_fusion.2), channel_id=1, replica_groups=mesh['grp'=4,'sub'=8] {'sub'}, dimensions={0}, use_global_device_ids=true | all-gather | bytes 589824 | tf_op jit(solution)/shard_map/all_gather | solution.py:72
  139.7 1.8 convolution_multiply_fusion.1
  141.5 1.3 copy.85
  142.8 2.5 copy.86
  145.3 9.4 %all_gather.47 = f32[512,128]{1,0:T(8,128)S(1)} all-gather(f32[128,128]{1,0:T(8,128)S(1)} %add_add_fusion.2), channel_id=1, replica_groups=mesh['grp'=4,'sub'=8] {'grp'}, dimensions={0}, use_global_device_ids=true | all-gather | bytes 327680 | tf_op jit(solution)/shard_map/all_gather | solution.py:61
  154.7 3.2 convolution_bitcast_fusion.1
  158.0 3.2 copy.110
  161.2 1.2 bitcast_reduce_fusion.2
  162.5 2.0 convolution_bitcast_fusion.3
  164.5 7.2 %fusion.42 = f32[2,1024,128]{1,2,0:T(8,128)S(1)} fusion(f32[2,1024,128]{1,2,0:T(8,128)} %copy.86, f32[128,512,1]{1,0,2:T(8,128)S(1)} %convolution_bitcast_fusion.3, f32[1,2,1024,512]{3,2,1,0:T(8,128)} %param.15, f32[1,2,1024,128]{2,3,1,0:T(8,128)} %copy-done.6, f32[2,1024]{1,0:T(2,128)S(1)} %compare_convert_fusion), kind=kOutput, calls=%fused_computation.29 | convolution fusion | flops 1611399168 | bytes 7610368 | tf_op jit(solution)/shard_map/jrs,sl->jrl/dot_general | solution.py:77
  171.7 11.4 %fusion.63 = f32[2,1024,128]{1,2,0:T(8,128)S(1)} fusion(f32[2,1024,128]{1,2,0:T(8,128)S(1)} %fusion.42, f32[1,2,1024,1024]{3,2,1,0:T(8,128)} %param.14, f32[2,1024]{1,0:T(2,128)S(1)} %compare_convert_fusion), kind=kOutput, calls=%fused_computation.39 | convolution fusion | flops 3221487616 | bytes 10493952 | tf_op jit(solution)/shard_map/jrc,jcl->jrl/dot_general | solution.py:79
  183.1 1.0 copy-done.11
  184.1 3.2 fusion.72
  187.3 2.5 copy.88
  189.8 2.4 reshape.166
  192.2 2.5 fusion.83
  194.7 1.2 copy.90
  195.9 4.2 %all-to-all-start.1 = ((f32[8,2,128,128]{3,2,1,0:T(8,128)}), f32[8,2,128,128]{3,2,1,0:T(8,128)}, u32[]{:S(2)}, u32[]{:S(2)}) async-start(f32[8,2,128,128]{3,2,1,0:T(8,128)} %copy.90), calls=%async_computation.3 | async-start | bytes 2097152 | tf_op jit(solution)/shard_map/all_to_all | solution.py:92
  200.9 36.7 %all-to-all-done.1 = f32[8,2,128,128]{3,2,1,0:T(8,128)} async-done(((f32[8,2,128,128]{3,2,1,0:T(8,128)}), f32[8,2,128,128]{3,2,1,0:T(8,128)}, u32[]{:S(2)}, u32[]{:S(2)}) %all-to-all-start.1) | async-done | bytes 1048608 | tf_op jit(solution)/shard_map/all_to_all | solution.py:92
  237.6 1.3 reduce_sum.67
  239.7 0.9 add_add_fusion.1
  240.6 14.8 %all_gather.48 = f32[1024,128]{0,1:T(8,128)S(1)} all-gather(f32[128,128]{0,1:T(8,128)S(1)} %add_add_fusion.1), channel_id=1, replica_groups=mesh['grp'=4,'sub'=8] {'sub'}, dimensions={0}, use_global_device_ids=true | all-gather | bytes 589824 | tf_op jit(solution)/shard_map/all_gather | solution.py:72
  255.4 0.9 copy.113
  256.3 2.0 copy.93
  258.3 2.1 convolution_multiply_fusion
  260.4 1.3 copy.94
  261.7 2.5 copy.95
  264.3 10.5 %all_gather.51 = f32[512,128]{0,1:T(8,128)S(1)} all-gather(f32[128,128]{0,1:T(8,128)S(1)} %add_add_fusion.1), channel_id=1, replica_groups=mesh['grp'=4,'sub'=8] {'grp'}, dimensions={0}, use_global_device_ids=true | all-gather | bytes 327680 | tf_op jit(solution)/shard_map/all_gather | solution.py:61
  274.7 3.1 convolution_bitcast_fusion
  278.0 3.4 copy.112
  282.8 4.5 %fusion.33 = f32[2,1024,128]{1,2,0:T(8,128)S(1)} fusion(f32[2,1024,128]{1,2,0:T(8,128)S(1)} %copy-done.12, f32[128,512,1]{1,0,2:T(8,128)S(1)} %convolution_bitcast_fusion.2, f32[1,2,1024,512]{3,2,1,0:T(8,128)S(1)} %copy-done.3, f32[1,2,1024,128]{2,3,1,0:T(8,128)S(1)} %copy-done.7, f32[2,1024]{1,0:T(2,128)S(1)} %compare_convert_fusion), kind=kOutput, calls=%fused_computation.26 | convolution fusion | flops 1611399168 | bytes 7610368 | tf_op jit(solution)/shard_map/jrs,sl->jrl/dot_general | solution.py:77
  287.2 11.4 %fusion.66 = f32[2,128,1024]{2,1,0:T(8,128)S(1)} fusion(f32[2,1024,128]{1,2,0:T(8,128)S(1)} %fusion.33, f32[1,2,1024,1024]{3,2,1,0:T(8,128)} %param.14, f32[2,1024]{1,0:T(2,128)S(1)} %compare_convert_fusion), kind=kOutput, calls=%fused_computation.40 | convolution fusion | flops 3221487616 | bytes 10493952 | tf_op jit(solution)/shard_map/jrc,jcl->jrl/dot_general | solution.py:79
  298.6 1.0 copy-done.4
  299.6 3.2 fusion.75
  302.8 2.6 copy.97
  305.3 2.4 reshape.169
  307.7 2.4 fusion.81
  310.2 1.2 copy.99
  311.4 4.6 %all-to-all-start.2 = ((f32[8,2,128,128]{3,2,1,0:T(8,128)}), f32[8,2,128,128]{3,2,1,0:T(8,128)}, u32[]{:S(2)}, u32[]{:S(2)}) async-start(f32[8,2,128,128]{3,2,1,0:T(8,128)} %copy.99), calls=%async_computation.5 | async-start | bytes 2097152 | tf_op jit(solution)/shard_map/all_to_all | solution.py:92
  315.9 1.3 copy.102
  317.3 40.5 %all-to-all-done.2 = f32[8,2,128,128]{3,2,1,0:T(8,128)} async-done(((f32[8,2,128,128]{3,2,1,0:T(8,128)}), f32[8,2,128,128]{3,2,1,0:T(8,128)}, u32[]{:S(2)}, u32[]{:S(2)}) %all-to-all-start.2) | async-done | bytes 1048608 | tf_op jit(solution)/shard_map/all_to_all | solution.py:92
  357.8 1.3 reduce_sum.69
  361.4 3.2 copy.114
  365.2 1.8 fusion.87
  (85 shorter events, 9.6 us)
Async XLA Ops:
  7.2 11.0 %copy-start = (f32[1024,512]{1,0:T(8,128)S(1)}, f32[1024,512]{1,0:T(8,128)}, u32[]{:S(2)}) copy-start(f32[1024,512]{1,0:T(8,128)} %param.13) | copy-start | bytes 6291460
  7.2 30.5 %copy-start.20 = (s32[1,2,8,1]{2,3,1,0:T(1,128)S(1)}, s32[1,2,8,1]{2,3,1,0:T(1,128)}, u32[]{:S(2)}) copy-start(s32[1,2,8,1]{2,3,1,0:T(1,128)} %param.25) | copy-start | bytes 196
  7.2 31.2 %copy-start.22 = (s32[1,2]{1,0:T(1,128)S(1)}, s32[1,2]{1,0:T(1,128)}, u32[]{:S(2)}) copy-start(s32[1,2]{1,0:T(1,128)} %param.24) | copy-start | bytes 28
  7.2 31.3 %copy-start.15 = (f32[1,2,8,128]{3,2,1,0:T(8,128)S(1)}, f32[1,2,8,128]{3,2,1,0:T(8,128)}, u32[]{:S(2)}) copy-start(f32[1,2,8,128]{3,2,1,0:T(8,128)} %param.21) | copy-start | bytes 24580
  7.2 115.0 %reduce-scatter.4.cloned.1.call-start = ((), (), s32[]{:S(2)}) async-start(), calls=%async_computation.6 | async-start | bytes 589824 | tf_op jit(solution)/shard_map/reduce_scatter | solution.py:66
  20.8 23.9 %copy-start.21 = (s32[1,2]{1,0:T(1,128)S(1)}, s32[1,2]{1,0:T(1,128)}, u32[]{:S(2)}) copy-start(s32[1,2]{1,0:T(1,128)} %param.23) | copy-start | bytes 28
  20.8 137.2 %all-gather.9.cloned.1.call-start = ((), (), s32[]{:S(2)}) async-start(), calls=%async_computation.9 | async-start | bytes 2359296 | tf_op jit(solution)/shard_map/all_gather | solution.py:81
  38.4 33.8 %copy-start.19 = (s32[16]{0:T(128)}, s32[16]{0:T(128)S(1)}, u32[]{:S(2)}) copy-start(s32[16]{0:T(128)S(1)} %eq.58) | copy-start | bytes 196
  46.3 18.7 %copy-start.6 = (f32[1,2,1024,128]{2,3,1,0:T(8,128)}, f32[1,2,1024,128]{2,3,1,0:T(8,128)S(1)}, u32[]{:S(2)}) copy-start(f32[1,2,1024,128]{2,3,1,0:T(8,128)S(1)} %copy.75) | copy-start | bytes 3145732
  53.6 12.4 %copy-start.1 = (f32[1,2,1024,512]{3,2,1,0:T(8,128)S(1)}, f32[1,2,1024,512]{3,2,1,0:T(8,128)}, u32[]{:S(2)}) copy-start(f32[1,2,1024,512]{3,2,1,0:T(8,128)} %param.15) | copy-start | bytes 12582916
  65.1 1.0 copy-start.10
  66.0 6.1 %copy-start.16 = (f32[1,2,8,128]{3,2,1,0:T(8,128)S(1)}, f32[1,2,8,128]{3,2,1,0:T(8,128)}, u32[]{:S(2)}) copy-start(f32[1,2,8,128]{3,2,1,0:T(8,128)} %param.22) | copy-start | bytes 24580
  72.2 4.0 %copy-start.17 = (s32[16]{0:T(128)}, s32[16]{0:T(128)S(1)}, u32[]{:S(2)}) copy-start(s32[16]{0:T(128)S(1)} %multiply_add_fusion.1) | copy-start | bytes 196
  76.2 44.1 %all-to-all-start = ((f32[8,2,128,128]{3,2,1,0:T(8,128)}), f32[8,2,128,128]{3,2,1,0:T(8,128)}, u32[]{:S(2)}, u32[]{:S(2)}) async-start(f32[8,2,128,128]{3,2,1,0:T(8,128)} %copy.83), calls=%async_computation.1 | async-start | bytes 2097152 | tf_op jit(solution)/shard_map/all_to_all | solution.py:92
  81.5 81.0 %all-gather.11.cloned.1.call-start = ((), (), s32[]{:S(2)}) async-start(), calls=%async_computation.10 | async-start | bytes 1179648 | tf_op jit(solution)/shard_map/all_gather | solution.py:56
  82.2 157.5 %reduce-scatter.6.cloned.1.call-start = ((), (), s32[]{:S(2)}) async-start(), calls=%async_computation.7 | async-start | bytes 589824 | tf_op jit(solution)/shard_map/reduce_scatter | solution.py:66
  157.9 120.0 %all-gather.13.cloned.1.call-start = ((), (), s32[]{:S(2)}) async-start(), calls=%async_computation.11 | async-start | bytes 2359296 | tf_op jit(solution)/shard_map/all_gather | solution.py:81
  171.7 12.4 %copy-start.2 = (f32[1,2,1024,512]{3,2,1,0:T(8,128)S(1)}, f32[1,2,1024,512]{3,2,1,0:T(8,128)}, u32[]{:S(2)}) copy-start(f32[1,2,1024,512]{3,2,1,0:T(8,128)} %param.15) | copy-start | bytes 12582916
  183.1 1.0 copy-start.11
  192.2 8.0 %copy-start.14 = (f32[128,128]{1,0:T(8,128)S(1)}, f32[128,128]{1,0:T(8,128)}, u32[]{:S(2)}) copy-start(f32[128,128]{1,0:T(8,128)} %param.19) | copy-start | bytes 196612
  195.9 41.7 %all-to-all-start.1 = ((f32[8,2,128,128]{3,2,1,0:T(8,128)}), f32[8,2,128,128]{3,2,1,0:T(8,128)}, u32[]{:S(2)}, u32[]{:S(2)}) async-start(f32[8,2,128,128]{3,2,1,0:T(8,128)} %copy.90), calls=%async_computation.3 | async-start | bytes 2097152 | tf_op jit(solution)/shard_map/all_to_all | solution.py:92
  200.1 159.7 %reduce-scatter.8.cloned.1.call-start = ((), (), s32[]{:S(2)}) async-start(), calls=%async_computation.8 | async-start | bytes 589824 | tf_op jit(solution)/shard_map/reduce_scatter | solution.py:66
  277.9 83.6 %all-gather.15.cloned.1.call-start = ((), (), s32[]{:S(2)}) async-start(), calls=%async_computation.12 | async-start | bytes 2359296 | tf_op jit(solution)/shard_map/all_gather | solution.py:81
  277.9 4.1 %copy-start.8 = (f32[1,512,512]{1,2,0:T(8,128)S(1)}, f32[1,512,512]{1,2,0:T(8,128)}, u32[]{:S(2)}) copy-start(f32[1,512,512]{1,2,0:T(8,128)} %all-gather.11.cloned.1.call-done) | copy-start | bytes 3145732
  277.9 4.8 %copy-start.3 = (f32[1,2,1024,512]{3,2,1,0:T(8,128)S(1)}, f32[1,2,1024,512]{3,2,1,0:T(8,128)}, u32[]{:S(2)}) copy-start(f32[1,2,1024,512]{3,2,1,0:T(8,128)} %param.15) | copy-start | bytes 12582916
  278.0 4.8 %copy-start.7 = (f32[1,2,1024,128]{2,3,1,0:T(8,128)S(1)}, f32[1,2,1024,128]{2,3,1,0:T(8,128)}, u32[]{:S(2)}) copy-start(f32[1,2,1024,128]{2,3,1,0:T(8,128)} %copy-done.6) | copy-start | bytes 3145732
  278.0 4.8 %copy-start.12 = (f32[2,1024,128]{1,2,0:T(8,128)S(1)}, f32[2,1024,128]{1,2,0:T(8,128)}, u32[]{:S(2)}) copy-start(f32[2,1024,128]{1,2,0:T(8,128)} %copy.95) | copy-start | bytes 3145732
  298.6 1.0 copy-start.4
  299.6 8.2 %copy-start.18 = (s32[16]{0:T(128)S(1)}, s32[16]{0:T(128)}, u32[]{:S(2)}) copy-start(s32[16]{0:T(128)} %copy-done.17) | copy-start | bytes 196
  310.2 5.8 %copy-start.5 = (f32[2,128,1024]{2,1,0:T(8,128)S(1)}, f32[2,128,1024]{2,1,0:T(8,128)}, u32[]{:S(2)}) copy-start(f32[2,128,1024]{2,1,0:T(8,128)} %copy-done.4) | copy-start | bytes 3145732
  310.2 49.6 %copy-start.13 = (f32[128,128]{0,1:T(8,128)S(1)}, f32[128,128]{0,1:T(8,128)}, u32[]{:S(2)}) copy-start(f32[128,128]{0,1:T(8,128)} %copy.87) | copy-start | bytes 196612
  311.4 46.4 %all-to-all-start.2 = ((f32[8,2,128,128]{3,2,1,0:T(8,128)}), f32[8,2,128,128]{3,2,1,0:T(8,128)}, u32[]{:S(2)}, u32[]{:S(2)}) async-start(f32[8,2,128,128]{3,2,1,0:T(8,128)} %copy.99), calls=%async_computation.5 | async-start | bytes 2097152 | tf_op jit(solution)/shard_map/all_to_all | solution.py:92
  317.2 47.9 %copy-start.9 = (f32[1,512,512]{1,2,0:T(8,128)S(1)}, f32[1,512,512]{1,2,0:T(8,128)}, u32[]{:S(2)}) copy-start(f32[1,512,512]{1,2,0:T(8,128)} %all-gather.11.cloned.1.call-done) | copy-start | bytes 3145732
Sparse Core Ops, SparseCore 0:
  20.9 31.7 reduce-scatter.3
  69.4 41.6 all-gather.8
  112.7 29.4 all-gather.10
  158.0 29.3 reduce-scatter.5
  188.9 37.8 all-gather.12
  278.0 29.1 reduce-scatter.7
  308.8 46.7 all-gather.14
